TPU v7x, 32 devices: a whole 2x2x4 slice. The times are simulated.
32 devices in a mesh: tm: 8 (over z, x), gz: 4 (over y, core).
Axes of the slice: x: 2, y: 2, z: 4, core: 2. Of those that a mesh axis runs over, the one named last changes fastest.
Arguments:
- source: float32 [16, 32, 32, 512], P('tm', None, None, 'gz'), may hold values from -8 to 8
- initial_guess: float32 [16, 32, 32, 512], P('tm', None, None, 'gz'), may hold values from -8 to 8
- diffusivity: float32 [32, 32, 512], P(None, None, 'gz'), may hold values from 0.25 to 2.5
Outputs:
- solution: float32 [16, 32, 32, 512], P('tm', None, None, 'gz')
- residual: float32 [16, 32, 32, 512], P('tm', None, None, 'gz')
All inputs are finite; a program needn't handle non-finite values.
Results may differ from a plain program's by a relative error of at most 0.00002.
Values sent between devices are 32-bit elements; how exact they have to be, the bound alone decides.
A program may use at most 128 MiB of HBM per device.

v0:
```python
import jax
import jax.numpy as jnp
from jax import lax
from jax.experimental import pallas as pl
from jax.experimental.pallas import tpu as pltpu
from jax.sharding import PartitionSpec as P

LEVELS = 5
damping = 0.8
base_coef = 8.0
F32 = jnp.float32
MESH = pl.DeviceIdType.MESH
PAD = 8


def make(mesh, nt, nx, ny, nz):
    ntm, ngz = mesh.shape["tm"], mesh.shape["gz"]
    group = 2 ** (LEVELS - 1) // nt
    groups = ntm // group
    half = group // 2
    xb = nx // group
    yp = ny + 2 * PAD
    hi0 = nz // 2
    times = [0] + [group // 2**l for l in range(LEVELS - 1)]
    versions = [0] + [4] * (LEVELS - 2) + [3]
    n_coarse = sum(versions)

    def kernel(src, guess, dif_hbm, sol, res, *scr):
        scr = list(scr)
        V = [scr.pop(0) for _ in range(6)]
        PV = [scr.pop(0) for _ in range(6)]
        f, dif, S0, rb, g1, es, rout = [scr.pop(0) for _ in range(7)]
        A = [None] + [[scr.pop(0) for _ in range(versions[l])] for l in range(1, LEVELS)]
        G = [None] + [scr.pop(0) for _ in range(1, LEVELS)]
        E = [None] + [scr.pop(0) for _ in range(1, LEVELS)]
        S = [S0] + [scr.pop(0) for _ in range(1, LEVELS)]
        ZS, ZL, ZR = [scr.pop(0) for _ in range(3)]
        (load_sem, out_sem, zsend, zlr, zrr, xsend, xlr, xrr, usend, urecv,
         asend, arecv, esend, erecv, psend, precv, tsend, trecv) = scr

        tm, gz = lax.axis_index("tm"), lax.axis_index("gz")
        grp, i = lax.div(tm, group), lax.rem(tm, group)

        def pos_of(k):
            return jnp.where(lax.rem(k, 2) == 0, lax.div(k, 2), group - 1 - lax.div(k, 2))

        def index_of(p):
            return jnp.where(p < half, 2 * p, 2 * (group - 1 - p) + 1)

        p = pos_of(i)
        center = pl.ds(PAD, ny)

        loads = [
            pltpu.make_async_copy(guess, V[0].at[:, pl.ds(1, nx), center, :], load_sem.at[0]),
            pltpu.make_async_copy(src, f, load_sem.at[1]),
            pltpu.make_async_copy(dif_hbm, dif, load_sem.at[2]),
        ]
        for c in loads:
            c.start()

        zpad = jnp.zeros((PAD, nz), F32)
        zrow = jnp.zeros((ny, nz), F32)

        for t in range(nt):
            def clear0(x, _, t=t):
                for v in V:
                    v[t, x, pl.ds(0, PAD), :] = zpad
                    v[t, x, pl.ds(PAD + ny, PAD), :] = zpad
                return 0
            lax.fori_loop(0, nx + 2, clear0, 0)
            for v in V:
                v[t, 0, center, :] = zrow
                v[t, nx + 1, center, :] = zrow
        for l in range(1, LEVELS):
            def clear1(t, _, l=l):
                for a in A[l]:
                    for x in range(xb + 2):
                        a[t, x] = jnp.zeros((yp, nz), F32)
                return 0
            lax.fori_loop(0, times[l] + 1, clear1, 0)

        @pl.when(tm == 0)
        def _():
            def clear2(x, _):
                for v in PV:
                    v[x] = zrow
                return 0
            lax.fori_loop(0, nx, clear2, 0)

        def clear3(n, _):
            ZL[n] = zrow
            ZR[n] = zrow
            return 0
        lax.fori_loop(0, 12 + n_coarse, clear3, 0)

        bar = pltpu.get_barrier_semaphore()

        def greet(where):
            pl.semaphore_signal(bar, inc=1, device_id=where, device_id_type=MESH)

        for j in range(1, group):
            greet({"tm": grp * group + lax.rem(i + j, group)})
        met = group - 1
        for d in (-1, 1):
            there = (gz + d >= 0) & (gz + d < ngz)
            met = met + jnp.where(there, 1, 0)

            @pl.when(there)
            def _(d=d):
                greet({"gz": gz + d})
        if groups > 1:
            for d in (-1, 1):
                there = (grp + d >= 0) & (grp + d < groups)
                met = met + jnp.where(there, group, 0)

                @pl.when(there)
                def _(d=d):
                    for j in range(group):
                        greet({"tm": (grp + d) * group + j})
        pl.semaphore_wait(bar, met)

        def remote(s, d, ss, rs, where):
            return pltpu.make_async_remote_copy(
                src_ref=s, dst_ref=d, send_sem=ss, recv_sem=rs, device_id=where, device_id_type=MESH)

        def step_copy(n, source):
            return remote(source, PV[n], usend.at[n], urecv.at[n], {"tm": tm + 1})

        def step_send(n, source):
            @pl.when(tm < ntm - 1)
            def _():
                step_copy(n, source).start()

        def step_recv(n, source):
            @pl.when(tm > 0)
            def _():
                step_copy(n, source).wait_recv()

        def step_sent(n, source):
            @pl.when(tm < ntm - 1)
            def _():
                step_copy(n, source).wait_send()

        def z_copies(n):
            par = n % 2
            return (remote(ZS.at[n], ZR.at[n], zsend.at[0, par], zrr.at[n], {"gz": gz - 1}),
                    remote(ZS.at[n], ZL.at[n], zsend.at[1, par], zlr.at[n], {"gz": gz + 1}))

        def z_send(n):
            lo, hi = z_copies(n)

            @pl.when(gz > 0)
            def _():
                lo.start()

            @pl.when(gz < ngz - 1)
            def _():
                hi.start()

        def z_wait(n):
            lo, hi = z_copies(n)

            @pl.when(gz > 0)
            def _():
                lo.wait_send()
                hi.wait_recv()

            @pl.when(gz < ngz - 1)
            def _():
                hi.wait_send()
                lo.wait_recv()

        lane = lax.broadcasted_iota(jnp.int32, (ny, nz), 1)

        def pack(acc, val, k):
            acc = jnp.where(lane == k, pltpu.roll(val, k, 1), acc)
            return jnp.where(lane == hi0 + k, pltpu.roll(val, lax.rem(k + hi0 + 1, nz), 1), acc)

        def flux(v, t, x, n, k):
            c = v[t, x, center, :]
            nb = v[t, x + 1, center, :] + v[t, x - 1, center, :]
            nb = nb + v[t, x, pl.ds(PAD + 1, ny), :] + v[t, x, pl.ds(PAD - 1, ny), :]
            left = jnp.where(lane == 0, pltpu.roll(ZL[n], hi0 - k, 1), pltpu.roll(c, 1, 1))
            right = jnp.where(lane == nz - 1, pltpu.roll(ZR[n], nz - 1 - k, 1), pltpu.roll(c, nz - 1, 1))
            return c, 6.0 * c - (nb + right + left)

        def defect(v, t, x, n, k, before, target, d, coef):
            c, lap = flux(v, t, x, n, k)
            return c, target - (coef * (c - before) + d * lap)

        def run(count, fn, n):
            def step(k, acc):
                return pack(acc, fn(k), k)
            ZS[n] = lax.fori_loop(0, count, step, zrow, unroll=2)
            z_send(n)

        def each(count, fn):
            def step(k, _):
                fn(k)
                return 0
            lax.fori_loop(0, count, step, 0, unroll=2)

        def before0(m, pn, t, x):
            return PV[pn][x] if t == 0 else V[m][t - 1, x + 1, center, :]

        def sweep0(m, t):
            n = 2 * m + t

            def fn(x):
                c, r = defect(V[m], t, x + 1, n, x, before0(m, m, t, x), f[t, x], dif[x], base_coef)
                new = c + S0[x] * r
                V[m + 1][t, x + 1, center, :] = new
                return new
            run(nx, fn, n + 2)

        def resid0(m, t, put):
            n = 2 * m + t

            def fn(x):
                _, r = defect(V[m], t, x + 1, n, x, before0(m, m, t, x), f[t, x], dif[x], base_coef)
                put(x, r)
            each(nx, fn)

        last = nt - 1

        def block(m):
            return V[m].at[last, pl.ds(1, nx), center, :]

        step_send(0, guess.at[last])
        for c in loads:
            c.wait()

        for t in (1, 0):
            def first(x, t=t):
                return V[0][t, x + 1, center, :]
            run(nx, first, t)

        def scales(x):
            S0[x] = damping / (base_coef + 6.0 * dif[x])
        each(nx, scales)
        for l in range(1, LEVELS):
            for x in range(xb):
                S[l][x] = damping / (base_coef / 2.0**l + 6.0 * dif[p * xb + x])

        z_wait(1)
        sweep0(0, 1)
        step_send(1, block(1))
        step_recv(0, guess.at[last])
        z_wait(0)
        sweep0(0, 0)
        z_wait(3)
        sweep0(1, 1)
        step_send(2, block(2))
        step_recv(1, block(1))
        z_wait(2)
        sweep0(1, 0)

        def put_rb(x, r):
            rb[x] = r
        z_wait(5)
        resid0(2, 1, put_rb)
        z_wait(4)
        step_recv(2, block(2))

        def put_g(x, r):
            g1[x] = (r + rb[x]) * 0.5
        resid0(2, 0, put_g)
        step_sent(0, guess.at[last])
        step_sent(1, block(1))
        step_sent(2, block(2))

        def a2a(j, to):
            other = lax.rem(i + j, group)
            return remote(g1.at[pl.ds(pos_of(other) * xb, xb)], G[1].at[to], asend.at[j], arecv.at[j],
                          {"tm": grp * group + other})

        for j in range(1, group):
            a2a(j, i).start()
        for x in range(xb):
            G[1][i, x] = g1[p * xb + x]
        for j in range(1, group):
            c = a2a(j, lax.rem(i + group - j, group))
            c.wait_recv()
            c.wait_send()

        slot = [0]

        def halo_copies(l, ver, n):
            a, T = A[l][ver], times[l]
            steps = pl.ds(1, T)
            lo = remote(a.at[steps, 1, center, :], a.at[steps, xb + 1, center, :],
                        xsend.at[0], xrr.at[n], {"tm": grp * group + index_of(lax.max(p - 1, 0))})
            hi = remote(a.at[steps, xb, center, :], a.at[steps, 0, center, :],
                        xsend.at[1], xlr.at[n], {"tm": grp * group + index_of(lax.min(p + 1, group - 1))})
            nxt = None
            if groups > 1:
                nxt = remote(a.at[T, pl.ds(1, xb), center, :], a.at[0, pl.ds(1, xb), center, :],
                             tsend.at[0], trecv.at[n], {"tm": tm + group})
            return lo, hi, nxt

        def fill(l, ver, fn):
            n = slot[0]
            slot[0] += 1
            T = times[l]
            a = A[l][ver]

            def put(k):
                t, x = lax.div(k, xb), lax.rem(k, xb)
                val = fn(t, x, k)
                a[t + 1, x + 1, center, :] = val
                return val
            run(T * xb, put, 12 + n)
            lo, hi, nxt = halo_copies(l, ver, n)

            @pl.when(p > 0)
            def _():
                lo.start()

            @pl.when(p < group - 1)
            def _():
                hi.start()
            if nxt is not None:
                @pl.when(grp < groups - 1)
                def _():
                    nxt.start()
            z_wait(12 + n)

            @pl.when(p > 0)
            def _():
                lo.wait_send()
                hi.wait_recv()

            @pl.when(p < group - 1)
            def _():
                hi.wait_send()
                lo.wait_recv()
            if nxt is not None:
                @pl.when(grp < groups - 1)
                def _():
                    nxt.wait_send()

                @pl.when(grp > 0)
                def _():
                    nxt.wait_recv()
            return 12 + n

        def defect_at(l, ver, n, t, x, k):
            a = A[l][ver]
            return defect(a, t + 1, x + 1, n, k, a[t, x + 1, center, :], G[l][t, x], dif[p * xb + x],
                          base_coef / 2.0**l)

        def relaxed(l, ver, n):
            def fn(t, x, k):
                c, r = defect_at(l, ver, n, t, x, k)
                return c + S[l][x] * r
            return fn

        def finish(l, ver, n):
            fn = relaxed(l, ver, n)

            def put(k):
                t, x = lax.div(k, xb), lax.rem(k, xb)
                E[l][t, x] = fn(t, x, k)
            each(times[l] * xb, put)

        def coarse(l):
            n = fill(l, 0, lambda t, x, k: S[l][x] * G[l][t, x])
            n = fill(l, 1, relaxed(l, 0, n))
            if l == LEVELS - 1:
                n = fill(l, 2, relaxed(l, 1, n))
                finish(l, 2, n)
                return

            def down(k):
                t, x = lax.div(k, xb), lax.rem(k, xb)
                _, ra = defect_at(l, 1, n, 2 * t, x, 2 * t * xb + x)
                _, rc = defect_at(l, 1, n, 2 * t + 1, x, (2 * t + 1) * xb + x)
                G[l + 1][t, x] = (ra + rc) * 0.5
            each(times[l + 1] * xb, down)
            coarse(l + 1)
            n = fill(l, 2, lambda t, x, k: A[l][1][t + 1, x + 1, center, :] + E[l + 1][lax.div(t, 2), x])
            n = fill(l, 3, relaxed(l, 2, n))
            finish(l, 3, n)

        coarse(1)

        ep = PV[5]

        def back(j, at):
            other = lax.rem(i + j, group)
            return remote(E[1].at[other], es.at[pl.ds(at * xb, xb)], esend.at[j], erecv.at[j],
                          {"tm": grp * group + other})

        def ahead(j, at):
            other = lax.rem(i + j, group)
            return other, remote(E[1].at[lax.rem(other + group - 1, group)], ep.at[pl.ds(at * xb, xb)],
                                 psend.at[j], precv.at[j],
                                 {"tm": jnp.where(other == 0, grp + 1, grp) * group + other})

        for j in range(1, group):
            back(j, p).start()
        for j in range(group):
            other, c = ahead(j, p)
            if j > 0:
                @pl.when(other > 0)
                def _(c=c):
                    c.start()
            if groups > 1:
                @pl.when((other == 0) & (grp < groups - 1))
                def _(c=c):
                    c.start()
        for x in range(xb):
            es[p * xb + x] = E[1][i, x]

        @pl.when(i > 0)
        def _():
            for x in range(xb):
                ep[p * xb + x] = E[1][lax.max(i - 1, 0), x]
        for j in range(1, group):
            back(j, pos_of(lax.rem(i + group - j, group))).wait_recv()

        for t in (1, 0):
            def lift(x, t=t):
                val = V[2][t, x + 1, center, :] + es[x]
                V[3][t, x + 1, center, :] = val
                return val
            run(nx, lift, 6 + t)
        z_wait(7)
        sweep0(3, 1)
        step_send(3, block(4))
        for j in range(group):
            _, c = ahead(j, pos_of(lax.rem(i + group - j, group)))
            if j > 0:
                @pl.when(i > 0)
                def _(c=c):
                    c.wait_recv()
            if groups > 1:
                @pl.when((i == 0) & (grp > 0))
                def _(c=c):
                    c.wait_recv()

        def lift_prev(x):
            rb[x] = PV[2][x] + ep[x]
        each(nx, lift_prev)
        z_wait(6)

        def sweep_a(m, prev):
            n = 2 * m

            def fn(x):
                c, r = defect(V[m], 0, x + 1, n, x, prev[x], f[0, x], dif[x], base_coef)
                new = c + S0[x] * r
                V[m + 1][0, x + 1, center, :] = new
                return new
            run(nx, fn, n + 2)

        sweep_a(3, rb)
        z_wait(9)
        sweep0(4, 1)
        step_send(4, block(5))
        outs = [pltpu.make_async_copy(V[5].at[t, pl.ds(1, nx), center, :], sol.at[t], out_sem.at[t])
                for t in range(nt)]
        outs[1].start()
        step_recv(3, block(4))
        z_wait(8)
        sweep_a(4, PV[3])
        outs[0].start()
        z_wait(11)

        def put_r(t):
            def put(x, r):
                rout[t, x] = r
            return put
        resid0(5, 1, put_r(1))
        rcopy = [pltpu.make_async_copy(rout.at[t], res.at[t], out_sem.at[nt + t]) for t in range(nt)]
        rcopy[1].start()
        z_wait(10)
        step_recv(4, block(5))

        def last_res(x):
            _, r = defect(V[5], 0, x + 1, 10, x, PV[4][x], f[0, x], dif[x], base_coef)
            rout[0, x] = r
        each(nx, last_res)
        rcopy[0].start()
        step_sent(3, block(4))
        step_sent(4, block(5))
        for j in range(1, group):
            back(j, p).wait_send()
        for j in range(group):
            other, c = ahead(j, p)
            if j > 0:
                @pl.when(other > 0)
                def _(c=c):
                    c.wait_send()
            if groups > 1:
                @pl.when((other == 0) & (grp < groups - 1))
                def _(c=c):
                    c.wait_send()
        for c in outs + rcopy:
            c.wait()

    full = pltpu.VMEM((nx, ny, nz), F32)
    dma = pltpu.SemaphoreType.DMA
    nzs = 12 + n_coarse
    scratch = [pltpu.VMEM((nt, nx + 2, yp, nz), F32)] * 6 + [full] * 6
    scratch += [pltpu.VMEM((nt, nx, ny, nz), F32), full, full, full, full, full, pltpu.VMEM((nt, nx, ny, nz), F32)]
    for l in range(1, LEVELS):
        scratch += [pltpu.VMEM((times[l] + 1, xb + 2, yp, nz), F32)] * versions[l]
    scratch += [pltpu.VMEM((times[l], xb, ny, nz), F32) for l in range(1, LEVELS)] * 2
    scratch += [pltpu.VMEM((xb, ny, nz), F32)] * (LEVELS - 1)
    scratch += [pltpu.VMEM((nzs, ny, nz), F32)] * 3
    scratch += [dma((3,)), dma((2 * nt,)), dma((2, 2)), dma((nzs,)), dma((nzs,)), dma((2,)), dma((n_coarse,)),
                dma((n_coarse,)), dma((5,)), dma((5,))] + [dma((group,))] * 6 + [dma((1,)), dma((n_coarse,))]
    shape = jax.ShapeDtypeStruct((nt, nx, ny, nz), F32)
    anyspec = pl.BlockSpec(memory_space=pl.ANY)
    return pl.pallas_call(
        kernel,
        out_shape=(shape, shape),
        in_specs=[anyspec] * 3,
        out_specs=(anyspec, anyspec),
        scratch_shapes=scratch,
        compiler_params=pltpu.CompilerParams(collective_id=0, has_side_effects=True, vmem_limit_bytes=56 << 20),
    )


def solution(mesh):
    def body(source, initial_guess, diffusivity):
        return make(mesh, *source.shape)(source, initial_guess, diffusivity)

    placed = (P("tm", None, None, "gz"), P("tm", None, None, "gz"), P(None, None, "gz"))
    return jax.shard_map(
        body,
        mesh=mesh,
        in_specs=placed,
        out_specs=(P("tm", None, None, "gz"), P("tm", None, None, "gz")),
        check_vma=False,
    )
```

profile of v0, /device:TPU:25, one launch (start us, length us, event | category | flops | bytes accessed | tf_op | source)
XLA Modules:
  0.0 178.0 jit_solution(13508870728868036581)
XLA Ops:
  0.6 174.0 %shard_map.50 = (f32[2,32,32,128]{3,2,1,0:T(8,128)}, f32[2,32,32,128]{3,2,1,0:T(8,128)}) custom-call(f32[2,32,32,128]{3,2,1,0:T(8,128)} %src.1, f32[2,32,32,128]{3,2,1,0:T(8,128)} %guess.1, f32[32,32,128]{2,1,0:T(8,128)} %dif_hbm.1), custom_call_target="tpu_custom_call" | custom-call | tf_op jit(solution)/shard_map/pallas_call | solution.py:528
  174.7 0.0 copy-start
  174.7 2.4 %copy.7 = f32[2,32,32,128]{3,2,1,0:T(8,128)} copy(f32[2,32,32,128]{3,2,1,0:T(8,128)} %get-tuple-element.4) | data formatting | bytes 2097152
  177.0 0.0 copy-done
  177.0 1.0 copy.8
Async XLA Ops:
  174.7 2.4 %copy-start = (f32[2,32,32,128]{3,2,1,0:T(8,128)S(1)}, f32[2,32,32,128]{3,2,1,0:T(8,128)}, u32[]{:S(2)}) copy-start(f32[2,32,32,128]{3,2,1,0:T(8,128)} %get-tuple-element.5) | copy-start | bytes 3145732
where the time goes:
time: 181 us; the launch traced here: 178 us
  Pallas kernels  174 us (96%)
  local copies, waits for them, and re-layouts  3.32 us (2%)
    pallas_call x1, Pallas kernels, body(): return make(mesh, *source.shape)(source, initial_guess, diffusivity)  174 us

commit v1 on v0

v1 whole, which is shorter than its diff:
```python
import jax
import jax.numpy as jnp
from jax import lax
from jax.experimental import pallas as pl
from jax.experimental.pallas import tpu as pltpu
from jax.sharding import PartitionSpec as P

LEVELS = 5
damping = 0.8
keep = 1.0 - damping
base_coef = 8.0
F32 = jnp.float32
MESH = pl.DeviceIdType.MESH
LANES = 128
PAD = 8
PX = 4
R = 8
D0 = 8
D1 = 24


def make(mesh, nt, nx, ny, nz):
    ntm, ngz = mesh.shape["tm"], mesh.shape["gz"]
    group = 2 ** (LEVELS - 1) // nt
    groups = ntm // group
    xb = nx // group
    yp = ny + 2 * PAD
    xp = nx + 2 * PX
    rb = LANES // ny
    C = nx // R
    nblk = nx // rb
    times = [0] + [group // 2**l for l in range(LEVELS - 1)]
    hx = [0] + [2] * (LEVELS - 2) + [3]
    xr = [xb + 2 * h for h in hx]
    last = nt - 1

    def kernel(src, guess, dif_hbm, sol, res, *scr):
        scr = list(scr)
        VA, VB, VC, F, DIF, S0, HG, HF, HD = [scr.pop(0) for _ in range(9)]
        rout, es, g1 = HG, HF, HD
        PV = [scr.pop(0) for _ in range(6)]
        PSs, PSr, ZSs, ZSr, DSs, DSr, GSs, GSr, ESs, ESr = [scr.pop(0) for _ in range(10)]
        A = [None] + [[scr.pop(0) for _ in range(3)] for l in range(1, LEVELS)]
        G = [None] + [scr.pop(0) for _ in range(1, LEVELS)]
        E = [None] + [scr.pop(0) for _ in range(1, LEVELS)]
        S = [S0] + [scr.pop(0) for _ in range(1, LEVELS)]
        LP = [None] + [scr.pop(0) for _ in range(1, LEVELS - 1)]
        (load_sem, out_sem, zs_s, zs_r, d_s, d_r, swap_s, swap_r, a_s, a_r, b_s, b_r,
         x_s, x_r, g_s, g_r, t_s, t_r, o_s, o_r) = scr

        tm, gz = lax.axis_index("tm"), lax.axis_index("gz")
        q_t, q_z = lax.rem(tm, 2), lax.rem(gz, 2)
        swapped = q_t != q_z
        stays = q_t == q_z
        I, s = tm - q_t + q_z, gz - q_z + q_t
        grp, i = lax.div(I, group), lax.rem(I, group)
        center = pl.ds(PAD, ny)
        lane = lax.broadcasted_iota(jnp.int32, (ny, nz), 1)
        m0, m1 = lane == 0, lane == nz - 1
        flip = {"tm": tm + 1 - 2 * q_t, "gz": gz + 1 - 2 * q_z}
        mate = {"tm": tm, "gz": gz + 1 - 2 * q_z}

        def holder(ii, ss):
            a, b = lax.rem(ii, 2), lax.rem(ss, 2)
            return {"tm": ii - a + b, "gz": ss - b + a}

        def remote(a, b, ss, rs, where):
            return pltpu.make_async_remote_copy(
                src_ref=a, dst_ref=b, send_sem=ss, recv_sem=rs, device_id=where, device_id_type=MESH)

        sends = []

        def start(cond, c):
            @pl.when(cond)
            def _():
                c.start()
            sends.append((cond, c))

        def recv(cond, c):
            @pl.when(cond)
            def _():
                c.wait_recv()

        def each(count, fn, unroll=1):
            whole = count // unroll

            def steps(k, _):
                for u in range(unroll):
                    fn(k * unroll + u)
                return 0
            lax.fori_loop(0, whole, steps, 0)
            for k in range(whole * unroll, count):
                fn(k)

        home = [pltpu.make_async_copy(guess, HG, load_sem.at[0]),
                pltpu.make_async_copy(src, HF, load_sem.at[1]),
                pltpu.make_async_copy(dif_hbm, HD, load_sem.at[2])]
        for c in (home[2], home[0], home[1]):
            c.start()

        zrow = jnp.zeros((ny, nz), F32)
        zpad = jnp.zeros((PAD, nz), F32)

        def clear_edges(x):
            for v in PV:
                for h in range(2):
                    v[h, x] = zrow
                    v[h, PX + nx + x] = zrow
        each(PX, clear_edges)

        bar = pltpu.get_barrier_semaphore()
        met = [jnp.int32(0)]

        def greet(cond, where):
            @pl.when(cond)
            def _():
                pl.semaphore_signal(bar, inc=1, device_id=where, device_id_type=MESH)
            met[0] = met[0] + jnp.where(cond, 1, 0)

        greet(tm >= 0, mate)
        greet(swapped, flip)
        for d in (-1, 1):
            greet((gz + d >= 0) & (gz + d < ngz), holder(tm, gz + d))
            greet((s + d >= 0) & (s + d < ngz), {"tm": I, "gz": s + d})
            greet((s + d >= 0) & (s + d < ngz), holder(I, s + d))
            greet((I + d >= 0) & (I + d < ntm), holder(I + d, s))
            if groups > 1:
                greet((grp + d >= 0) & (grp + d < groups), holder(I + d * group, s))
        for j in range(1, group):
            greet(tm >= 0, holder(grp * group + lax.rem(i + j, group), s))
        pl.semaphore_wait(bar, met[0])

        moves = []
        for j in range(C):
            rows = pl.ds(R * j, R)
            there = pl.ds(PX + R * j, R)
            for k, (h, v) in enumerate(((guess.at[:, rows], VA.at[:, 0, there, center]),
                                        (src.at[:, rows], F.at[:, 0, there]))):
                n = 2 * j + k
                far = remote(h, v, swap_s.at[n], swap_r.at[n], flip)
                near = pltpu.make_async_copy(h, v, load_sem.at[3 + n])
                start(swapped, far)

                @pl.when(stays)
                def _(near=near):
                    near.start()
                moves.append((far, near))
        dif_own = pltpu.make_async_copy(dif_hbm, DIF.at[0, pl.ds(PX, nx)], load_sem.at[3 + 2 * C])
        dif_far = remote(dif_hbm, DIF.at[0, pl.ds(PX, nx)], swap_s.at[2 * C], swap_r.at[2 * C], mate)
        start(stays, dif_far)

        @pl.when(stays)
        def _():
            dif_own.start()

        def moved(n):
            far, near = moves[n]
            recv(swapped, far)

            @pl.when(stays)
            def _():
                near.wait()

        def clear_v(x):
            for v in (VA, VB, VC):
                for t in range(nt):
                    for h in range(2):
                        v[t, h, x, pl.ds(0, PAD), :] = zpad
                        v[t, h, x, pl.ds(PAD + ny, PAD), :] = zpad
        each(xp, clear_v)

        def clear_x(x):
            for xx in (x, PX + nx + x):
                for h in range(2):
                    for t in range(nt):
                        for v in (VA, VB, VC):
                            v[t, h, xx, center, :] = zrow
                        F[t, h, xx] = zrow
                    DIF[h, xx] = zrow
        each(PX, clear_x)

        @pl.when(I == 0)
        def _():
            def clear_p(x):
                for v in PV:
                    for h in range(2):
                        v[h, PX + x] = zrow
            each(nx, clear_p)
        for l in range(1, LEVELS):
            def clear_a(t, l=l):
                for h in range(2):
                    for a in A[l]:
                        for x in range(xr[l]):
                            a[t + 1, h, x, pl.ds(0, PAD), :] = zpad
                            a[t + 1, h, x, pl.ds(PAD + ny, PAD), :] = zpad
                    for x in range(hx[l]):
                        for xx in (x, hx[l] + xb + x):
                            G[l][t, h, xx] = zrow
                            A[l][1][t + 1, h, xx, center, :] = zrow
            each(times[l], clear_a)

            @pl.when(grp == 0)
            def _(l=l):
                def clear_b(x):
                    for h in range(2):
                        for a in A[l]:
                            a[0, h, x, center, :] = zrow
                each(xr[l], clear_b)

        def pack(block, depth):
            tr = block.reshape(rb * ny, nz).T
            return tr[:depth], tr[nz - depth:]

        def unpack(lo, hi, depth):
            mid = jnp.zeros((nz - 2 * depth, LANES), F32)
            return jnp.concatenate([lo, mid, hi], axis=0).T.reshape(rb, ny, nz)

        for side, edge in ((0, s == ngz - 1), (1, s == 0)):
            @pl.when(edge)
            def _(side=side):
                for z in (ZSr, DSr, GSr):
                    def clear_z(k, z=z):
                        z[side, k] = jnp.zeros(z.shape[2:], F32)
                    each(z.shape[1], clear_z)

        home[2].wait()

        def pack_d(b):
            lo, hi = pack(HD[pl.ds(b * rb, rb)], D1)
            DSs[0, b] = lo
            DSs[1, b] = hi
        each(nblk, pack_d, 2)
        home[0].wait()
        home[1].wait()

        def pack_h(b):
            for k, h in enumerate((HG, HF)):
                for t in range(nt):
                    lo, hi = pack(h[t, pl.ds(b * rb, rb)], D0)
                    n = (k * nt + t) * nblk + b
                    ZSs[0, n] = lo
                    ZSs[1, n] = hi
        each(nblk, pack_h)

        def z_pair(side, a, b, n, home_side):
            d = -1 if side == 0 else 1
            to = holder(tm, gz + d) if home_side else holder(I, s + d)
            c = remote(a.at[side], b.at[side], zs_s.at[n], zs_r.at[n], to)
            base = gz if home_side else s
            can_send = (base + d >= 0) & (base + d < ngz)
            can_recv = (s - d >= 0) & (s - d < ngz)
            return can_send, can_recv, c

        zc = [z_pair(side, a, b, 2 * k + side, True) for k, (a, b) in enumerate(((DSs, DSr), (ZSs, ZSr))) for side in range(2)]
        for cs, cr, c in zc:
            start(cs, c)

        @pl.when(stays)
        def _():
            dif_own.wait()
        recv(swapped, dif_far)
        for cs, cr, c in zc[:2]:
            recv(cr, c)

        def unpack_d(b):
            DIF[1, pl.ds(PX + b * rb, rb)] = unpack(DSr[0, b], DSr[1, b], D1)
        each(nblk, unpack_d, 2)

        def scales(x):
            for h in range(2):
                S0[h, x] = damping / (base_coef + 6.0 * DIF[h, x])
        each(xp, scales)
        row0 = [i * xb + PX - h for h in hx]
        for l in range(1, LEVELS):
            def scales_l(x, l=l):
                for h in range(2):
                    S[l][h, x] = damping / (base_coef / 2.0**l + 6.0 * DIF[h, row0[l] + x])
            each(xr[l], scales_l)
        for cs, cr, c in zc[2:]:
            recv(cr, c)

        def unpack_h(b):
            for t in range(nt):
                VA[t, 1, pl.ds(PX + b * rb, rb), center, :] = unpack(ZSr[0, t * nblk + b], ZSr[1, t * nblk + b], D0)
                F[t, 1, pl.ds(PX + b * rb, rb)] = unpack(ZSr[0, (nt + t) * nblk + b], ZSr[1, (nt + t) * nblk + b], D0)
        each(nblk, unpack_h)

        def gather(v, t, x, parts):
            c = [v[t, h, x, center, :] for h in range(2)]
            up = [pltpu.roll(a, 1, 1) for a in c]
            dn = [pltpu.roll(a, nz - 1, 1) for a in c]
            nb = []
            for h in range(parts):
                a = v[t, h, x + 1, center, :] + v[t, h, x - 1, center, :]
                a = a + (v[t, h, x, pl.ds(PAD + 1, ny), :] + v[t, h, x, pl.ds(PAD - 1, ny), :])
                nb.append(a + (jnp.where(m0, up[1 - h], up[h]) + jnp.where(m1, dn[1 - h], dn[h])))
            return c, nb

        def relax(v, w, t, pv, lo, n):
            def fn(k):
                x = PX + lo + k
                c, nb = gather(v, t, x, 2)
                for h in range(2):
                    b = pv[h, x] if t == 0 else v[t - 1, h, x, center, :]
                    w[t, h, x, center, :] = keep * c[h] + S0[h, x] * ((F[t, h, x] + base_coef * b) + DIF[h, x] * nb[h])
            each(n, fn, 2)

        def residual(v, pv, lo, n, put):
            def fn(k):
                x = PX + lo + k
                d = DIF[0, x]
                rs = []
                b = pv[0, x]
                for t in range(nt):
                    c, nb = gather(v, t, x, 1)
                    rs.append((F[t, 0, x] + base_coef * b) + d * nb[0] - (base_coef + 6.0 * d) * c[0])
                    b = c[0]
                put(lo + k, rs)
            each(n, fn, 2)

        def span(j, off):
            lo = R * j - off
            return lo, (R if j < C - 1 or off == 0 else R + rb)

        def d_copies(n, v, j, off):
            lo, m = span(j, off)
            rows = pl.ds(PX + lo, m)
            k = n * C + j
            bl = pl.ds(j * (R // rb), m // rb)
            own = remote(v.at[last, 0, rows, center], PV[n].at[0, rows], d_s.at[0, k], d_r.at[0, k], holder(I + 1, s))
            halo = remote(PSs.at[n, bl], PSr.at[n, bl], d_s.at[1, k], d_r.at[1, k], holder(I + 1, s))
            return own, halo

        def d_send(n, v, j, off):
            lo, m = span(j, off)

            def fn(b):
                lo8, hi8 = pack(v[last, 1, pl.ds(PX + lo + b * rb, rb), center, :], D0)
                PSs[n, j * (R // rb) + b, pl.ds(0, D0)] = lo8
                PSs[n, j * (R // rb) + b, pl.ds(D0, D0)] = hi8
            each(m // rb, fn, 2)
            own, halo = d_copies(n, v, j, off)
            start(I < ntm - 1, own)
            start(I < ntm - 1, halo)

        def d_recv(n, v, j, off):
            lo, m = span(j, off)
            own, halo = d_copies(n, v, j, off)

            @pl.when(I > 0)
            def _():
                own.wait_recv()
                halo.wait_recv()

                def fn(b):
                    k = j * (R // rb) + b
                    PV[n][1, pl.ds(PX + lo + b * rb, rb)] = unpack(PSr[n, k, pl.ds(0, D0)], PSr[n, k, pl.ds(D0, D0)], D0)
                each(m // rb, fn, 2)

        def phase(v, w, u, n, arrive, put, after2, after_r):
            for j in range(C + 2):
                if j < C:
                    arrive(j)
                    d_send(n, v, j, 0)
                    for t in range(nt - 1, 0, -1):
                        relax(v, w, t, None, *span(j, 1))
                    d_send(n + 1, w, j, 1)
                if 1 <= j <= C:
                    d_recv(n, v, j - 1, 0)
                    relax(v, w, 0, PV[n], *span(j - 1, 1))
                    for t in range(nt - 1, 0, -1):
                        relax(w, u, t, None, *span(j - 1, 2))
                    d_send(n + 2, u, j - 1, 2)
                    d_recv(n + 1, w, j - 1, 1)
                    relax(w, u, 0, PV[n + 1], *span(j - 1, 2))
                    after2(j - 1)
                if j >= 2:
                    d_recv(n + 2, u, j - 2, 2)
                    lo = max(R * (j - 2) - 3, 0)
                    hi = R * (j - 1) - 3 if j - 2 < C - 1 else nx
                    residual(u, PV[n + 2], lo, hi - lo, put)
                    after_r(j - 2, lo, hi)

        def a2a(o, at):
            return remote(g1.at[pl.ds(o * xb, xb)], G[1].at[at, 0, pl.ds(hx[1], xb)], a_s.at[o], a_r.at[at], holder(grp * group + o, s))

        def arrive_in(j):
            moved(2 * j)
            moved(2 * j + 1)

        def put_g(x, rs):
            g1[x] = (rs[0] + rs[1]) * 0.5

        done = [0]

        def spread(j, lo, hi):
            while done[0] < group and (done[0] + 1) * xb <= hi:
                o = done[0]
                start(i != o, a2a(o, i))

                @pl.when(i == o)
                def _(o=o):
                    for x in range(xb):
                        G[1][i, 0, hx[1] + x] = g1[o * xb + x]
                done[0] += 1

        phase(VA, VB, VC, 0, arrive_in, put_g, lambda j: None, spread)

        for o in range(group):
            recv(i != o, a2a(o, o))
        turn = {"x": 0, "t": 0}

        bpr = xb // rb

        def g_strip(k):
            t, b = lax.div(k, bpr), lax.rem(k, bpr)
            lo, hi = pack(G[1][t, 0, pl.ds(hx[1] + b * rb, rb)], D1)
            GSs[0, k] = lo
            GSs[1, k] = hi
        each(times[1] * bpr, g_strip, 2)
        gc = [z_pair(side, GSs, GSr, 4 + side, False) for side in range(2)]
        for cs, cr, c in gc:
            start(cs, c)
        for cs, cr, c in gc:
            recv(cr, c)

        def g_unstrip(k):
            t, b = lax.div(k, bpr), lax.rem(k, bpr)
            G[1][t, 1, pl.ds(hx[1] + b * rb, rb)] = unpack(GSr[0, k], GSr[1, k], D1)
        each(times[1] * bpr, g_unstrip, 2)

        def x_halo(at, H, depth):
            n = turn["x"]
            turn["x"] += 1
            lo = remote(at(pl.ds(H, depth)), at(pl.ds(H + xb, depth)), x_s.at[0, n], x_r.at[0, n], holder(I - 1, s))
            hi = remote(at(pl.ds(H + xb - depth, depth)), at(pl.ds(H - depth, depth)), x_s.at[1, n], x_r.at[1, n],
                        holder(I + 1, s))
            start(i > 0, lo)
            start(i < group - 1, hi)
            recv(i > 0, hi)
            recv(i < group - 1, lo)

        def t_halo(l, ver, depth, lifted=False):
            if groups == 1:
                return
            lo, n = hx[l] - depth, xb + 2 * depth
            k = turn["t"]
            turn["t"] += 1
            a, T = A[l][ver], times[l]
            rows = pl.ds(lo, n)
            to = LP[l].at[:, rows] if lifted else a.at[0, :, rows, center]
            c = remote(a.at[T, :, rows, center], to, t_s.at[k], t_r.at[k], holder(I + group, s))
            start(grp < groups - 1, c)
            recv(grp > 0, c)
            if lifted:
                @pl.when(grp > 0)
                def _():
                    for x in range(lo, lo + n):
                        for h in range(2):
                            a[0, h, x, center, :] = LP[l][h, x]

        def coarse_rows(l, lo, n, fn, steps=None):
            def step(t):
                for k in range(n):
                    fn(t, lo + k)
            each(times[l] if steps is None else steps, step)

        def first(l, depth):
            lo, n = hx[l] - depth, xb + 2 * depth

            def fn(t, x):
                for h in range(2):
                    A[l][0][t + 1, h, x, center, :] = S[l][h, x] * G[l][t, h, x]
            coarse_rows(l, lo, n, fn)
            t_halo(l, 0, depth)

        def relaxed(l, ver, depth, put):
            a = A[l][ver]
            coef = base_coef / 2.0**l

            def fn(t, x):
                c, nb = gather(a, t + 1, x, 2)
                for h in range(2):
                    b = a[t, h, x, center, :]
                    put(t, h, x, keep * c[h] + S[l][h, x] * ((G[l][t, h, x] + coef * b) + DIF[h, row0[l] + x] * nb[h]))
            coarse_rows(l, hx[l] - depth, xb + 2 * depth, fn)

        def into(l, ver):
            def put(t, h, x, val):
                A[l][ver][t + 1, h, x, center, :] = val
            return put

        def finish(l):
            def put(t, h, x, val):
                E[l][t, h, x - hx[l]] = val
            return put

        def coarse(l):
            H = hx[l]
            x_halo(lambda rows: G[l].at[:, :, rows], H, H)
            first(l, H)
            if l == LEVELS - 1:
                relaxed(l, 0, 2, into(l, 1))
                t_halo(l, 1, 2)
                relaxed(l, 1, 1, into(l, 2))
                t_halo(l, 2, 1)
                relaxed(l, 2, 0, finish(l))
                return
            relaxed(l, 0, 1, into(l, 1))
            t_halo(l, 1, 1)
            coef = base_coef / 2.0**l

            def down(t, x):
                parts = []
                d = [DIF[h, row0[l] + x] for h in range(2)]
                for k in range(2):
                    c, nb = gather(A[l][1], 2 * t + k + 1, x, 2)
                    parts.append([(G[l][2 * t + k, h, x] + coef * A[l][1][2 * t + k, h, x, center, :]) + d[h] * nb[h]
                                  - (coef + 6.0 * d[h]) * c[h] for h in range(2)])
                for h in range(2):
                    G[l + 1][t, h, x - H + hx[l + 1]] = (parts[0][h] + parts[1][h]) * 0.5
            coarse_rows(l, H, xb, down, times[l + 1])
            coarse(l + 1)

            def lift(t, x):
                for h in range(2):
                    A[l][1][t + 1, h, x, center, :] = A[l][1][t + 1, h, x, center, :] + E[l + 1][lax.div(t, 2), h, x - H]
            coarse_rows(l, H, xb, lift)
            T = times[l]
            x_halo(lambda rows: A[l][1].at[pl.ds(1, T), :, rows, center], H, 2)
            t_halo(l, 1, 2, True)
            relaxed(l, 1, 1, into(l, 2))
            t_halo(l, 2, 1)
            relaxed(l, 2, 0, finish(l))

        coarse(1)

        def e_strip(k):
            t, b = lax.div(k, bpr), lax.rem(k, bpr)
            lo, hi = pack(E[1][t, 1, pl.ds(b * rb, rb)], D0)
            ESs[k, pl.ds(0, D0)] = lo
            ESs[k, pl.ds(D0, D0)] = hi
        each(times[1] * bpr, e_strip, 2)

        def back(other, at, j):
            to = holder(grp * group + other, s)
            return (remote(E[1].at[other, 0], es.at[0, pl.ds(at * xb, xb)], b_s.at[0, j], b_r.at[0, j], to),
                    remote(ESs.at[pl.ds(other * bpr, bpr)], ESr.at[pl.ds(at * bpr, bpr)], b_s.at[1, j], b_r.at[1, j], to))

        for j in range(1, group):
            for c in back(lax.rem(i + j, group), i, j):
                start(tm >= 0, c)
        for x in range(xb):
            es[0, i * xb + x] = E[1][i, 0, x]
        for b in range(bpr):
            ESr[i * bpr + b] = ESs[i * bpr + b]
        for j in range(1, group):
            for c in back(lax.rem(i + j, group), lax.rem(i + group - j, group), j):
                c.wait_recv()

        def arrive_up(j):
            def fn(b):
                k = j * (R // rb) + b
                es[1, pl.ds(k * rb, rb)] = unpack(ESr[k, pl.ds(0, D0)], ESr[k, pl.ds(D0, D0)], D0)
            each(R // rb, fn, 2)

            def lift(k):
                x = R * j + k
                for h in range(2):
                    e = es[h, x]
                    for t in range(nt):
                        VC[t, h, PX + x, center, :] = VC[t, h, PX + x, center, :] + e
            each(R, lift, 2)

        outs = []

        def emit(a, b, n):
            far = remote(a, b, o_s.at[n], o_r.at[n], flip)
            near = pltpu.make_async_copy(a, b, out_sem.at[n])
            start(swapped, far)

            @pl.when(stays)
            def _():
                near.start()
            outs.append((far, near))

        def emit_sol(j):
            lo, m = span(j, 2)
            hi = nx if j == C - 1 else lo + m
            lo = max(lo, 0)
            emit(VB.at[:, 0, pl.ds(PX + lo, hi - lo), center], sol.at[:, pl.ds(lo, hi - lo)], j)

        def put_r(x, rs):
            for t in range(nt):
                rout[t, x] = rs[t]

        def emit_res(j, lo, hi):
            emit(rout.at[:, pl.ds(lo, hi - lo)], res.at[:, pl.ds(lo, hi - lo)], C + j)

        for cond, c in sends:
            @pl.when(cond)
            def _(c=c):
                c.wait_send()
        sends.clear()
        phase(VC, VA, VB, 3, arrive_up, put_r, emit_sol, emit_res)
        for far, near in outs:
            recv(swapped, far)

            @pl.when(stays)
            def _(near=near):
                near.wait()
        for cond, c in sends:
            @pl.when(cond)
            def _(c=c):
                c.wait_send()

    dma = pltpu.SemaphoreType.DMA
    vm = lambda *shape: pltpu.VMEM(shape, F32)
    bpr = xb // rb
    n_t = 4 * (LEVELS - 2) + 3
    n_x = 2 * (LEVELS - 2) + 1
    scratch = [vm(nt, 2, xp, yp, nz)] * 3
    scratch += [vm(nt, 2, xp, ny, nz), vm(2, xp, ny, nz), vm(2, xp, ny, nz)]
    scratch += [vm(nt, nx, ny, nz), vm(nt, nx, ny, nz), vm(nx, ny, nz)]
    scratch += [vm(2, xp, ny, nz)] * 6
    scratch += [vm(6, nblk + 1, 2 * D0, LANES)] * 2
    scratch += [vm(2, 2 * nt * nblk, D0, LANES)] * 2
    scratch += [vm(2, nblk, D1, LANES)] * 2
    scratch += [vm(2, times[1] * bpr, D1, LANES)] * 2
    scratch += [vm(times[1] * bpr, 2 * D0, LANES), vm(nblk, 2 * D0, LANES)]
    for l in range(1, LEVELS):
        scratch += [vm(times[l] + 1, 2, xr[l], yp, nz)] * 3
    scratch += [vm(times[l], 2, xr[l], ny, nz) for l in range(1, LEVELS)]
    scratch += [vm(times[l], 2, xb, ny, nz) for l in range(1, LEVELS)]
    scratch += [vm(2, xr[l], ny, nz) for l in range(1, LEVELS)]
    scratch += [vm(2, xr[l], ny, nz) for l in range(1, LEVELS - 1)]
    scratch += [dma((3 + 2 * C + 1,)), dma((2 * C,)), dma((6,)), dma((6,)), dma((2, 6 * C)), dma((2, 6 * C)),
                dma((2 * C + 1,)), dma((2 * C + 1,)), dma((group,)), dma((group,)), dma((2, group)), dma((2, group)),
                dma((2, n_x)), dma((2, n_x)), dma((1,)), dma((1,)), dma((n_t,)), dma((n_t,)), dma((2 * C,)), dma((2 * C,))]
    shape = jax.ShapeDtypeStruct((nt, nx, ny, nz), F32)
    anyspec = pl.BlockSpec(memory_space=pl.ANY)
    return pl.pallas_call(
        kernel,
        out_shape=(shape, shape),
        in_specs=[anyspec] * 3,
        out_specs=(anyspec, anyspec),
        scratch_shapes=scratch,
        compiler_params=pltpu.CompilerParams(collective_id=0, has_side_effects=True, vmem_limit_bytes=63 << 20),
    )


def solution(mesh):
    def body(source, initial_guess, diffusivity):
        return make(mesh, *source.shape)(source, initial_guess, diffusivity)

    placed = (P("tm", None, None, "gz"), P("tm", None, None, "gz"), P(None, None, "gz"))
    return jax.shard_map(
        body,
        mesh=mesh,
        in_specs=placed,
        out_specs=(P("tm", None, None, "gz"), P("tm", None, None, "gz")),
        check_vma=False,
    )
```

time: 181 us -> 156 us (0.86)
  Pallas kernels: 174 us -> 149 us
    pallas_call x1, Pallas kernels: 174 us -> 149 us  [body(): return make(mesh, *source.shape)(source, initial_guess, diffusivity)]
where the time goes in v1:
time: 156 us; the launch traced here: 153 us
  Pallas kernels  149 us (96%)
  local copies, waits for them, and re-layouts  3.32 us (2%)
    pallas_call x1, Pallas kernels, body(): return make(mesh, *source.shape)(source, initial_guess, diffusivity)  149 us
    unnamed x4, local copies, waits for them, and re-layouts  3.32 us

profile of v1, /device:TPU:25, one launch (start us, length us, event | category | flops | bytes accessed | tf_op | source)
XLA Modules:
  0.0 152.9 jit_solution(8814565891311209753)
XLA Ops:
  0.6 149.0 %shard_map.50 = (f32[2,32,32,128]{3,2,1,0:T(8,128)}, f32[2,32,32,128]{3,2,1,0:T(8,128)}) custom-call(f32[2,32,32,128]{3,2,1,0:T(8,128)} %src.1, f32[2,32,32,128]{3,2,1,0:T(8,128)} %guess.1, f32[32,32,128]{2,1,0:T(8,128)} %dif_hbm.1), custom_call_target="tpu_custom_call" | custom-call | tf_op jit(solution)/shard_map/pallas_call | solution.py:654
  149.6 0.0 copy-start
  149.6 2.4 %copy.7 = f32[2,32,32,128]{3,2,1,0:T(8,128)} copy(f32[2,32,32,128]{3,2,1,0:T(8,128)} %get-tuple-element.4) | data formatting | bytes 2097152
  152.0 0.0 copy-done
  152.0 1.0 copy.8
Async XLA Ops:
  149.6 2.4 %copy-start = (f32[2,32,32,128]{3,2,1,0:T(8,128)S(1)}, f32[2,32,32,128]{3,2,1,0:T(8,128)}, u32[]{:S(2)}) copy-start(f32[2,32,32,128]{3,2,1,0:T(8,128)} %get-tuple-element.5) | copy-start | bytes 3145732

commit v2 on v1

--- a/solution.py
+++ b/solution.py
@@ -14,9 +14,9 @@
 LANES = 128
 PAD = 8
 PX = 4
-R = 8
 D0 = 8
-D1 = 24
+D1 = 16
+NP = 10
 
 
 def make(mesh, nt, nx, ny, nz):
@@ -27,7 +27,9 @@
     yp = ny + 2 * PAD
     xp = nx + 2 * PX
     rb = LANES // ny
-    C = nx // R
+    q = nx // 8
+    cuts = {"down": [0, 2 * q, 4 * q, 6 * q, nx], "up": [0, 2 * q, 4 * q, 6 * q, nx]}
+    C = len(cuts["down"]) - 1
     nblk = nx // rb
     times = [0] + [group // 2**l for l in range(LEVELS - 1)]
     hx = [0] + [2] * (LEVELS - 2) + [3]
@@ -36,17 +38,17 @@
 
     def kernel(src, guess, dif_hbm, sol, res, *scr):
         scr = list(scr)
-        VA, VB, VC, F, DIF, S0, HG, HF, HD = [scr.pop(0) for _ in range(9)]
+        VA, VB, VC, WA, WB, F, GL, DIF, S0, S1, HG, HF, HD, RB = [scr.pop(0) for _ in range(14)]
         rout, es, g1 = HG, HF, HD
-        PV = [scr.pop(0) for _ in range(6)]
-        PSs, PSr, ZSs, ZSr, DSs, DSr, GSs, GSr, ESs, ESr = [scr.pop(0) for _ in range(10)]
-        A = [None] + [[scr.pop(0) for _ in range(3)] for l in range(1, LEVELS)]
-        G = [None] + [scr.pop(0) for _ in range(1, LEVELS)]
-        E = [None] + [scr.pop(0) for _ in range(1, LEVELS)]
-        S = [S0] + [scr.pop(0) for _ in range(1, LEVELS)]
-        LP = [None] + [scr.pop(0) for _ in range(1, LEVELS - 1)]
+        PV = [scr.pop(0) for _ in range(NP)]
+        PSs, PSr, ZGs, ZGr, ZFs, ZFr, DSs, DSr, GSs, GSr, ESs, ESr = [scr.pop(0) for _ in range(12)]
+        A = [None] * 2 + [[scr.pop(0) for _ in range(3)] for l in range(2, LEVELS)]
+        G = [None] * 2 + [scr.pop(0) for _ in range(2, LEVELS)]
+        E = [None] * 2 + [scr.pop(0) for _ in range(2, LEVELS)]
+        S = [S0, S1] + [scr.pop(0) for _ in range(2, LEVELS)]
+        LP = [None] * 2 + [scr.pop(0) for _ in range(2, LEVELS - 1)]
         (load_sem, out_sem, zs_s, zs_r, d_s, d_r, swap_s, swap_r, a_s, a_r, b_s, b_r,
-         x_s, x_r, g_s, g_r, t_s, t_r, o_s, o_r) = scr
+         x_s, x_r, g_s, g_r, t_s, t_r, o_s, o_r, p_s, p_r, f_s, f_r) = scr
 
         tm, gz = lax.axis_index("tm"), lax.axis_index("gz")
         q_t, q_z = lax.rem(tm, 2), lax.rem(gz, 2)
@@ -59,6 +61,7 @@
         m0, m1 = lane == 0, lane == nz - 1
         flip = {"tm": tm + 1 - 2 * q_t, "gz": gz + 1 - 2 * q_z}
         mate = {"tm": tm, "gz": gz + 1 - 2 * q_z}
+        par, z = q_z, lax.div(i, 2)
 
         def holder(ii, ss):
             a, b = lax.rem(ii, 2), lax.rem(ss, 2)
@@ -128,14 +131,18 @@
                 greet((grp + d >= 0) & (grp + d < groups), holder(I + d * group, s))
         for j in range(1, group):
             greet(tm >= 0, holder(grp * group + lax.rem(i + j, group), s))
+            if j % 2 == 0:
+                for d in (-1, 1):
+                    greet((s + d >= 0) & (s + d < ngz), holder(grp * group + lax.rem(i + j, group), s + d))
         pl.semaphore_wait(bar, met[0])
 
-        moves = []
-        for j in range(C):
-            rows = pl.ds(R * j, R)
-            there = pl.ds(PX + R * j, R)
-            for k, (h, v) in enumerate(((guess.at[:, rows], VA.at[:, 0, there, center]),
-                                        (src.at[:, rows], F.at[:, 0, there]))):
+        moves = {}
+        for k in range(2):
+            for j in range(C):
+                first, many = cuts["down"][j], cuts["down"][j + 1] - cuts["down"][j]
+                rows, there = pl.ds(first, many), pl.ds(PX + first, many)
+                h, v = ((guess.at[:, rows], VA.at[:, 0, there, center]) if k == 0 else
+                        (src.at[:, rows], F.at[:, 0, there]))
                 n = 2 * j + k
                 far = remote(h, v, swap_s.at[n], swap_r.at[n], flip)
                 near = pltpu.make_async_copy(h, v, load_sem.at[3 + n])
@@ -144,7 +151,7 @@
                 @pl.when(stays)
                 def _(near=near):
                     near.start()
-                moves.append((far, near))
+                moves[n] = (far, near)
         dif_own = pltpu.make_async_copy(dif_hbm, DIF.at[0, pl.ds(PX, nx)], load_sem.at[3 + 2 * C])
         dif_far = remote(dif_hbm, DIF.at[0, pl.ds(PX, nx)], swap_s.at[2 * C], swap_r.at[2 * C], mate)
         start(stays, dif_far)
@@ -167,6 +174,10 @@
                     for h in range(2):
                         v[t, h, x, pl.ds(0, PAD), :] = zpad
                         v[t, h, x, pl.ds(PAD + ny, PAD), :] = zpad
+            for v in (WA, WB):
+                for h in range(2):
+                    v[0, h, x, pl.ds(0, PAD), :] = zpad
+                    v[0, h, x, pl.ds(PAD + ny, PAD), :] = zpad
         each(xp, clear_v)
 
         def clear_x(x):
@@ -176,7 +187,10 @@
                         for v in (VA, VB, VC):
                             v[t, h, xx, center, :] = zrow
                         F[t, h, xx] = zrow
+                    for v in (WA, WB):
+                        v[0, h, xx, center, :] = zrow
                     DIF[h, xx] = zrow
+                    GL[h, xx] = zrow
         each(PX, clear_x)
 
         @pl.when(I == 0)
@@ -186,7 +200,7 @@
                     for h in range(2):
                         v[h, PX + x] = zrow
             each(nx, clear_p)
-        for l in range(1, LEVELS):
+        for l in range(2, LEVELS):
             def clear_a(t, l=l):
                 for h in range(2):
                     for a in A[l]:
@@ -218,10 +232,10 @@
         for side, edge in ((0, s == ngz - 1), (1, s == 0)):
             @pl.when(edge)
             def _(side=side):
-                for z in (ZSr, DSr, GSr):
-                    def clear_z(k, z=z):
-                        z[side, k] = jnp.zeros(z.shape[2:], F32)
-                    each(z.shape[1], clear_z)
+                for a in (ZGr, ZFr, DSr, GSr):
+                    def clear_z(k, a=a):
+                        a[side, k] = jnp.zeros(a.shape[2:], F32)
+                    each(a.shape[1], clear_z)
 
         home[2].wait()
 
@@ -234,12 +248,11 @@
         home[1].wait()
 
         def pack_h(b):
-            for k, h in enumerate((HG, HF)):
+            for h, a, depth in ((HG, ZGs, D1), (HF, ZFs, D0)):
                 for t in range(nt):
-                    lo, hi = pack(h[t, pl.ds(b * rb, rb)], D0)
-                    n = (k * nt + t) * nblk + b
-                    ZSs[0, n] = lo
-                    ZSs[1, n] = hi
+                    lo, hi = pack(h[t, pl.ds(b * rb, rb)], depth)
+                    a[0, t * nblk + b] = lo
+                    a[1, t * nblk + b] = hi
         each(nblk, pack_h)
 
         def z_pair(side, a, b, n, home_side):
@@ -251,7 +264,7 @@
             can_recv = (s - d >= 0) & (s - d < ngz)
             return can_send, can_recv, c
 
-        zc = [z_pair(side, a, b, 2 * k + side, True) for k, (a, b) in enumerate(((DSs, DSr), (ZSs, ZSr))) for side in range(2)]
+        zc = [z_pair(side, a, b, 2 * k + side, True) for k, (a, b) in enumerate(((DSs, DSr), (ZGs, ZGr), (ZFs, ZFr))) for side in range(2)]
         for cs, cr, c in zc:
             start(cs, c)
 
@@ -269,21 +282,25 @@
         def scales(x):
             for h in range(2):
                 S0[h, x] = damping / (base_coef + 6.0 * DIF[h, x])
+                S1[h, x] = damping / (base_coef / 2.0 + 6.0 * DIF[h, x])
         each(xp, scales)
         row0 = [i * xb + PX - h for h in hx]
-        for l in range(1, LEVELS):
+        for l in range(2, LEVELS):
             def scales_l(x, l=l):
                 for h in range(2):
                     S[l][h, x] = damping / (base_coef / 2.0**l + 6.0 * DIF[h, row0[l] + x])
             each(xr[l], scales_l)
-        for cs, cr, c in zc[2:]:
+        for cs, cr, c in zc[2:4]:
             recv(cr, c)
 
-        def unpack_h(b):
+        def unpack_g(b):
             for t in range(nt):
-                VA[t, 1, pl.ds(PX + b * rb, rb), center, :] = unpack(ZSr[0, t * nblk + b], ZSr[1, t * nblk + b], D0)
-                F[t, 1, pl.ds(PX + b * rb, rb)] = unpack(ZSr[0, (nt + t) * nblk + b], ZSr[1, (nt + t) * nblk + b], D0)
-        each(nblk, unpack_h)
+                VA[t, 1, pl.ds(PX + b * rb, rb), center, :] = unpack(ZGr[0, t * nblk + b], ZGr[1, t * nblk + b], D1)
+        each(nblk, unpack_g, 2)
+
+        def unpack_f(b):
+            for t in range(nt):
+                F[t, 1, pl.ds(PX + b * rb, rb)] = unpack(ZFr[0, t * nblk + b], ZFr[1, t * nblk + b], D0)
 
         def gather(v, t, x, parts):
             c = [v[t, h, x, center, :] for h in range(2)]
@@ -296,56 +313,77 @@
                 nb.append(a + (jnp.where(m0, up[1 - h], up[h]) + jnp.where(m1, dn[1 - h], dn[h])))
             return c, nb
 
-        def relax(v, w, t, pv, lo, n):
+        fine = (lambda t, h, x: F[t, h, x], S0, base_coef)
+        second = (lambda t, h, x: GL[h, x], S1, base_coef / 2.0)
+
+        def relaxed_row(lev, v, t, pv, x):
+            g, sc, coef = lev
+            c, nb = gather(v, t, x, 2)
+            b = [pv[h, x] if t == 0 else v[t - 1, h, x, center, :] for h in range(2)]
+            return [keep * c[h] + sc[h, x] * ((g(t, h, x) + coef * b[h]) + DIF[h, x] * nb[h]) for h in range(2)]
+
+        def relax(lev, v, w, t, pv, lo, n):
             def fn(k):
                 x = PX + lo + k
-                c, nb = gather(v, t, x, 2)
-                for h in range(2):
-                    b = pv[h, x] if t == 0 else v[t - 1, h, x, center, :]
-                    w[t, h, x, center, :] = keep * c[h] + S0[h, x] * ((F[t, h, x] + base_coef * b) + DIF[h, x] * nb[h])
-            each(n, fn, 2)
-
-        def residual(v, pv, lo, n, put):
+                val = relaxed_row(lev, v, t, pv, x)
+                for h in range(2):
+                    w[t, h, x, center, :] = val[h]
+            each(n, fn, 8)
+
+        def residual(lev, v, steps, pv, lo, n, parts, put):
+            g, _, coef = lev
+
             def fn(k):
                 x = PX + lo + k
-                d = DIF[0, x]
+                d = [DIF[h, x] for h in range(parts)]
+                b = [pv[h, x] for h in range(parts)]
                 rs = []
-                b = pv[0, x]
-                for t in range(nt):
-                    c, nb = gather(v, t, x, 1)
-                    rs.append((F[t, 0, x] + base_coef * b) + d * nb[0] - (base_coef + 6.0 * d) * c[0])
-                    b = c[0]
+                for t in range(steps):
+                    c, nb = gather(v, t, x, parts)
+                    rs.append([(g(t, h, x) + coef * b[h]) + d[h] * nb[h] - (coef + 6.0 * d[h]) * c[h] for h in range(parts)])
+                    b = c
                 put(lo + k, rs)
-            each(n, fn, 2)
+            each(n, fn, 4 if parts * steps > 2 else 8)
+
+        B = list(cuts["down"])
 
         def span(j, off):
-            lo = R * j - off
-            return lo, (R if j < C - 1 or off == 0 else R + rb)
-
-        def d_copies(n, v, j, off):
+            hi = B[j + 1] - off if j < C - 1 else nx
+            if j == 0:
+                m = -(-hi // rb) * rb
+                return hi - m, m
+            return B[j] - off, -(-(hi - B[j] + off) // rb) * rb
+
+        def block0(j):
+            return B[j] // rb
+
+        def inside(j, off):
+            return max(B[j] - off, 0), (B[j + 1] - off if j < C - 1 else nx)
+
+        def d_copies(n, v, t, j, off):
             lo, m = span(j, off)
             rows = pl.ds(PX + lo, m)
             k = n * C + j
-            bl = pl.ds(j * (R // rb), m // rb)
-            own = remote(v.at[last, 0, rows, center], PV[n].at[0, rows], d_s.at[0, k], d_r.at[0, k], holder(I + 1, s))
+            bl = pl.ds(block0(j), m // rb)
+            own = remote(v.at[t, 0, rows, center], PV[n].at[0, rows], d_s.at[0, k], d_r.at[0, k], holder(I + 1, s))
             halo = remote(PSs.at[n, bl], PSr.at[n, bl], d_s.at[1, k], d_r.at[1, k], holder(I + 1, s))
             return own, halo
 
-        def d_send(n, v, j, off):
+        def d_send(n, v, t, j, off):
             lo, m = span(j, off)
 
             def fn(b):
-                lo8, hi8 = pack(v[last, 1, pl.ds(PX + lo + b * rb, rb), center, :], D0)
-                PSs[n, j * (R // rb) + b, pl.ds(0, D0)] = lo8
-                PSs[n, j * (R // rb) + b, pl.ds(D0, D0)] = hi8
-            each(m // rb, fn, 2)
-            own, halo = d_copies(n, v, j, off)
+                lo8, hi8 = pack(v[t, 1, pl.ds(PX + lo + b * rb, rb), center, :], D0)
+                PSs[n, block0(j) + b, pl.ds(0, D0)] = lo8
+                PSs[n, block0(j) + b, pl.ds(D0, D0)] = hi8
+            own, halo = d_copies(n, v, t, j, off)
             start(I < ntm - 1, own)
+            each(m // rb, fn, 3)
             start(I < ntm - 1, halo)
 
-        def d_recv(n, v, j, off):
+        def d_recv(n, v, t, j, off):
             lo, m = span(j, off)
-            own, halo = d_copies(n, v, j, off)
+            own, halo = d_copies(n, v, t, j, off)
 
             @pl.when(I > 0)
             def _():
@@ -353,81 +391,118 @@
                 halo.wait_recv()
 
                 def fn(b):
-                    k = j * (R // rb) + b
+                    k = block0(j) + b
                     PV[n][1, pl.ds(PX + lo + b * rb, rb)] = unpack(PSr[n, k, pl.ds(0, D0)], PSr[n, k, pl.ds(D0, D0)], D0)
-                each(m // rb, fn, 2)
-
-        def phase(v, w, u, n, arrive, put, after2, after_r):
-            for j in range(C + 2):
-                if j < C:
-                    arrive(j)
-                    d_send(n, v, j, 0)
-                    for t in range(nt - 1, 0, -1):
-                        relax(v, w, t, None, *span(j, 1))
-                    d_send(n + 1, w, j, 1)
-                if 1 <= j <= C:
-                    d_recv(n, v, j - 1, 0)
-                    relax(v, w, 0, PV[n], *span(j - 1, 1))
-                    for t in range(nt - 1, 0, -1):
-                        relax(w, u, t, None, *span(j - 1, 2))
-                    d_send(n + 2, u, j - 1, 2)
-                    d_recv(n + 1, w, j - 1, 1)
-                    relax(w, u, 0, PV[n + 1], *span(j - 1, 2))
-                    after2(j - 1)
-                if j >= 2:
-                    d_recv(n + 2, u, j - 2, 2)
-                    lo = max(R * (j - 2) - 3, 0)
-                    hi = R * (j - 1) - 3 if j - 2 < C - 1 else nx
-                    residual(u, PV[n + 2], lo, hi - lo, put)
-                    after_r(j - 2, lo, hi)
-
-        def a2a(o, at):
-            return remote(g1.at[pl.ds(o * xb, xb)], G[1].at[at, 0, pl.ds(hx[1], xb)], a_s.at[o], a_r.at[at], holder(grp * group + o, s))
-
-        def arrive_in(j):
-            moved(2 * j)
-            moved(2 * j + 1)
+                each(m // rb, fn, 3)
+
+        before = range(nt - 1, 0, -1)
 
         def put_g(x, rs):
-            g1[x] = (rs[0] + rs[1]) * 0.5
-
-        done = [0]
-
-        def spread(j, lo, hi):
-            while done[0] < group and (done[0] + 1) * xb <= hi:
-                o = done[0]
-                start(i != o, a2a(o, i))
+            for h in range(2):
+                g = (rs[0][h] + rs[1][h]) * 0.5
+                GL[h, PX + x] = g
+                WA[0, h, PX + x, center, :] = S1[h, PX + x] * g
+
+        def put_r1(x, rs):
+            g1[x] = rs[0][0]
+
+        bpr = xb // rb
+        buddy = holder(I + 1 - 2 * par, s)
+
+        def to_buddy(o):
+            rows = pl.ds(o * xb, xb)
+            return remote(g1.at[rows], RB.at[rows], p_s.at[o], p_r.at[o], buddy)
+
+        def to_owner(o, at):
+            return remote(g1.at[pl.ds(o * xb, xb)], G[2].at[at, 0, pl.ds(hx[2], xb)], a_s.at[o], a_r.at[at],
+                          holder(grp * group + o, s))
+
+        def strip_to(side, o, at):
+            d = -1 if side == 0 else 1
+            return remote(GSs.at[side, pl.ds(o * bpr, bpr)], GSr.at[side, pl.ds(at * bpr, bpr)], g_s.at[side, o],
+                          g_r.at[side, at], holder(grp * group + o, s + d))
+
+        ready, sent = [0], [0]
+
+        def offer(hi):
+            while ready[0] < group and (ready[0] + 1) * xb <= hi:
+                start(par != ready[0] % 2, to_buddy(ready[0]))
+                ready[0] += 1
+
+        def spread():
+            while sent[0] < ready[0]:
+                o = sent[0]
+                sent[0] += 1
+                mine = par == o % 2
+                recv(mine, to_buddy(o))
+
+                @pl.when(mine)
+                def _(o=o):
+                    def fn(b):
+                        rows = pl.ds(o * xb + b * rb, rb)
+                        g = (g1[rows] + RB[rows]) * 0.5
+                        g1[rows] = g
+                        lo, hi = pack(g, D1)
+                        GSs[0, o * bpr + b] = lo
+                        GSs[1, o * bpr + b] = hi
+                    each(bpr, fn)
+                start(mine & (i != o), to_owner(o, z))
+                start(mine & (s > 0), strip_to(0, o, z))
+                start(mine & (s < ngz - 1), strip_to(1, o, z))
 
                 @pl.when(i == o)
                 def _(o=o):
                     for x in range(xb):
-                        G[1][i, 0, hx[1] + x] = g1[o * xb + x]
-                done[0] += 1
-
-        phase(VA, VB, VC, 0, arrive_in, put_g, lambda j: None, spread)
-
-        for o in range(group):
-            recv(i != o, a2a(o, o))
+                        G[2][z, 0, hx[2] + x] = g1[o * xb + x]
+
+        for j in range(C):
+            moved(2 * j)
+            d_send(0, VA, last, j, 0)
+        for cs, cr, c in zc[4:]:
+            recv(cr, c)
+        each(nblk, unpack_f, 2)
+        for j in range(C + 3):
+            spread()
+            if 0 <= j - 3 < C:
+                k = j - 3
+                d_recv(4, WB, 0, k, 4)
+                lo, hi = inside(k, 5)
+                residual(second, WB, 1, PV[4], lo, hi - lo, 1, put_r1)
+                offer(hi)
+            if 0 <= j - 2 < C:
+                k = j - 2
+                d_recv(3, WA, 0, k, 3)
+                relax(second, WA, WB, 0, PV[3], *span(k, 4))
+                d_send(4, WB, 0, k, 4)
+            if 0 <= j - 1 < C:
+                k = j - 1
+                d_recv(1, VB, last, k, 1)
+                relax(fine, VB, VC, 0, PV[1], *span(k, 2))
+                d_recv(2, VC, last, k, 2)
+                residual(fine, VC, nt, PV[2], *span(k, 3), 2, put_g)
+                d_send(3, WA, 0, k, 3)
+            if j < C:
+                moved(2 * j + 1)
+                for t in before:
+                    relax(fine, VA, VB, t, None, *span(j, 1))
+                d_send(1, VB, last, j, 1)
+                d_recv(0, VA, last, j, 0)
+                relax(fine, VA, VB, 0, PV[0], *span(j, 1))
+                for t in before:
+                    relax(fine, VB, VC, t, None, *span(j, 2))
+                d_send(2, VC, last, j, 2)
+        spread()
+
+        for at in range(group // 2):
+            recv(z != at, to_owner(0, at))
+            recv(s < ngz - 1, strip_to(0, 0, at))
+            recv(s > 0, strip_to(1, 0, at))
         turn = {"x": 0, "t": 0}
-
-        bpr = xb // rb
-
-        def g_strip(k):
-            t, b = lax.div(k, bpr), lax.rem(k, bpr)
-            lo, hi = pack(G[1][t, 0, pl.ds(hx[1] + b * rb, rb)], D1)
-            GSs[0, k] = lo
-            GSs[1, k] = hi
-        each(times[1] * bpr, g_strip, 2)
-        gc = [z_pair(side, GSs, GSr, 4 + side, False) for side in range(2)]
-        for cs, cr, c in gc:
-            start(cs, c)
-        for cs, cr, c in gc:
-            recv(cr, c)
 
         def g_unstrip(k):
             t, b = lax.div(k, bpr), lax.rem(k, bpr)
-            G[1][t, 1, pl.ds(hx[1] + b * rb, rb)] = unpack(GSr[0, k], GSr[1, k], D1)
-        each(times[1] * bpr, g_unstrip, 2)
+            G[2][t, 1, pl.ds(hx[2] + b * rb, rb)] = unpack(GSr[0, k], GSr[1, k], D1)
+        each(times[2] * bpr, g_unstrip, 2)
 
         def x_halo(at, H, depth):
             n = turn["x"]
@@ -533,44 +608,75 @@
             t_halo(l, 2, 1)
             relaxed(l, 2, 0, finish(l))
 
-        coarse(1)
+        coarse(2)
+
+        def drain():
+            for cond, c in sends:
+                @pl.when(cond)
+                def _(c=c):
+                    c.wait_send()
+            sends.clear()
+        drain()
 
         def e_strip(k):
             t, b = lax.div(k, bpr), lax.rem(k, bpr)
-            lo, hi = pack(E[1][t, 1, pl.ds(b * rb, rb)], D0)
+            lo, hi = pack(E[2][t, 1, pl.ds(b * rb, rb)], D0)
             ESs[k, pl.ds(0, D0)] = lo
             ESs[k, pl.ds(D0, D0)] = hi
-        each(times[1] * bpr, e_strip, 2)
-
-        def back(other, at, j):
-            to = holder(grp * group + other, s)
-            return (remote(E[1].at[other, 0], es.at[0, pl.ds(at * xb, xb)], b_s.at[0, j], b_r.at[0, j], to),
-                    remote(ESs.at[pl.ds(other * bpr, bpr)], ESr.at[pl.ds(at * bpr, bpr)], b_s.at[1, j], b_r.at[1, j], to))
-
-        for j in range(1, group):
-            for c in back(lax.rem(i + j, group), i, j):
-                start(tm >= 0, c)
+        each(times[2] * bpr, e_strip, 2)
+
+        def back(zz, at):
+            to = holder(grp * group + 2 * zz + par, s)
+            return (remote(E[2].at[zz, 0], es.at[0, pl.ds(at * xb, xb)], b_s.at[0, zz], b_r.at[0, at], to),
+                    remote(ESs.at[pl.ds(zz * bpr, bpr)], ESr.at[pl.ds(at * bpr, bpr)], b_s.at[1, zz], b_r.at[1, at], to))
+
+        for zz in range(group // 2):
+            for c in back(zz, i):
+                start(z != zz, c)
         for x in range(xb):
-            es[0, i * xb + x] = E[1][i, 0, x]
+            es[0, i * xb + x] = E[2][z, 0, x]
         for b in range(bpr):
-            ESr[i * bpr + b] = ESs[i * bpr + b]
-        for j in range(1, group):
-            for c in back(lax.rem(i + j, group), lax.rem(i + group - j, group), j):
-                c.wait_recv()
+            ESr[i * bpr + b] = ESs[z * bpr + b]
+
+        B[:] = cuts["up"]
+        got = [0]
+
+        def pass_on(o):
+            rows, bl = pl.ds(o * xb, xb), pl.ds(o * bpr, bpr)
+            return (remote(es.at[0, rows], es.at[0, rows], f_s.at[0, o], f_r.at[0, o], buddy),
+                    remote(ESr.at[bl], ESr.at[bl], f_s.at[1, o], f_r.at[1, o], buddy))
 
         def arrive_up(j):
+            upto = min(group, -(-B[j + 1] // xb))
+            for o in range(got[0], upto):
+                for c in back(0, o):
+                    recv((par == o % 2) & (i != o), c)
+                for c in pass_on(o):
+                    start(par == o % 2, c)
+            for o in range(got[0], upto):
+                for c in pass_on(o):
+                    recv(par != o % 2, c)
+            got[0] = upto
+
             def fn(b):
-                k = j * (R // rb) + b
+                k = block0(j) + b
                 es[1, pl.ds(k * rb, rb)] = unpack(ESr[k, pl.ds(0, D0)], ESr[k, pl.ds(D0, D0)], D0)
-            each(R // rb, fn, 2)
+            each((B[j + 1] - B[j]) // rb, fn, 2)
 
             def lift(k):
-                x = R * j + k
-                for h in range(2):
-                    e = es[h, x]
+                x = B[j] + k
+                for h in range(2):
+                    WB[0, h, PX + x, center, :] = WB[0, h, PX + x, center, :] + es[h, x]
+            each(B[j + 1] - B[j], lift, 4)
+
+        def lift_fine(lo, n):
+            def fn(k):
+                x = PX + lo + k
+                e = relaxed_row(second, WA, 0, PV[6], x)
+                for h in range(2):
                     for t in range(nt):
-                        VC[t, h, PX + x, center, :] = VC[t, h, PX + x, center, :] + e
-            each(R, lift, 2)
+                        VC[t, h, x, center, :] = VC[t, h, x, center, :] + e[h]
+            each(n, fn, 8)
 
         outs = []
 
@@ -585,58 +691,82 @@
             outs.append((far, near))
 
         def emit_sol(j):
-            lo, m = span(j, 2)
-            hi = nx if j == C - 1 else lo + m
-            lo = max(lo, 0)
+            lo, hi = inside(j, 4)
             emit(VB.at[:, 0, pl.ds(PX + lo, hi - lo), center], sol.at[:, pl.ds(lo, hi - lo)], j)
 
         def put_r(x, rs):
             for t in range(nt):
-                rout[t, x] = rs[t]
+                rout[t, x] = rs[t][0]
 
         def emit_res(j, lo, hi):
             emit(rout.at[:, pl.ds(lo, hi - lo)], res.at[:, pl.ds(lo, hi - lo)], C + j)
 
-        for cond, c in sends:
-            @pl.when(cond)
-            def _(c=c):
-                c.wait_send()
-        sends.clear()
-        phase(VC, VA, VB, 3, arrive_up, put_r, emit_sol, emit_res)
+        for j in range(C + 4):
+            if 0 <= j - 4 < C:
+                k = j - 4
+                d_recv(9, VB, last, k, 4)
+                lo, hi = inside(k, 5)
+                residual(fine, VB, nt, PV[9], lo, hi - lo, 1, put_r)
+                emit_res(k, lo, hi)
+            if 0 <= j - 3 < C:
+                k = j - 3
+                d_recv(7, VC, last, k, 2)
+                relax(fine, VC, VA, 0, PV[7], *span(k, 3))
+                for t in before:
+                    relax(fine, VA, VB, t, None, *span(k, 4))
+                d_send(9, VB, last, k, 4)
+                d_recv(8, VA, last, k, 3)
+                relax(fine, VA, VB, 0, PV[8], *span(k, 4))
+                emit_sol(k)
+            if 0 <= j - 2 < C:
+                k = j - 2
+                d_recv(6, WA, 0, k, 1)
+                lift_fine(*span(k, 2))
+                d_send(7, VC, last, k, 2)
+                for t in before:
+                    relax(fine, VC, VA, t, None, *span(k, 3))
+                d_send(8, VA, last, k, 3)
+            if 0 <= j - 1 < C:
+                k = j - 1
+                d_recv(5, WB, 0, k, 0)
+                relax(second, WB, WA, 0, PV[5], *span(k, 1))
+                d_send(6, WA, 0, k, 1)
+            if j < C:
+                arrive_up(j)
+                d_send(5, WB, 0, j, 0)
         for far, near in outs:
             recv(swapped, far)
 
             @pl.when(stays)
             def _(near=near):
                 near.wait()
-        for cond, c in sends:
-            @pl.when(cond)
-            def _(c=c):
-                c.wait_send()
+        drain()
 
     dma = pltpu.SemaphoreType.DMA
     vm = lambda *shape: pltpu.VMEM(shape, F32)
     bpr = xb // rb
-    n_t = 4 * (LEVELS - 2) + 3
-    n_x = 2 * (LEVELS - 2) + 1
-    scratch = [vm(nt, 2, xp, yp, nz)] * 3
-    scratch += [vm(nt, 2, xp, ny, nz), vm(2, xp, ny, nz), vm(2, xp, ny, nz)]
-    scratch += [vm(nt, nx, ny, nz), vm(nt, nx, ny, nz), vm(nx, ny, nz)]
-    scratch += [vm(2, xp, ny, nz)] * 6
-    scratch += [vm(6, nblk + 1, 2 * D0, LANES)] * 2
-    scratch += [vm(2, 2 * nt * nblk, D0, LANES)] * 2
+    n_t = 4 * (LEVELS - 3) + 3
+    n_x = 2 * (LEVELS - 3) + 1
+    wide, flat = vm(nt, 2, xp, yp, nz), vm(2, xp, ny, nz)
+    one = vm(1, 2, xp, yp, nz)
+    scratch = [wide] * 3 + [one] * 2 + [vm(nt, 2, xp, ny, nz)] + [flat] * 4
+    scratch += [vm(nt, nx, ny, nz), vm(nt, nx, ny, nz), vm(nx, ny, nz), vm(nx, ny, nz)]
+    scratch += [flat] * NP
+    scratch += [vm(NP, nblk + 1, 2 * D0, LANES)] * 2
+    scratch += [vm(2, nt * nblk, D1, LANES)] * 2 + [vm(2, nt * nblk, D0, LANES)] * 2
     scratch += [vm(2, nblk, D1, LANES)] * 2
-    scratch += [vm(2, times[1] * bpr, D1, LANES)] * 2
-    scratch += [vm(times[1] * bpr, 2 * D0, LANES), vm(nblk, 2 * D0, LANES)]
-    for l in range(1, LEVELS):
+    scratch += [vm(2, nblk, D1, LANES), vm(2, times[2] * bpr, D1, LANES)]
+    scratch += [vm(times[2] * bpr, 2 * D0, LANES), vm(nblk, 2 * D0, LANES)]
+    for l in range(2, LEVELS):
         scratch += [vm(times[l] + 1, 2, xr[l], yp, nz)] * 3
-    scratch += [vm(times[l], 2, xr[l], ny, nz) for l in range(1, LEVELS)]
-    scratch += [vm(times[l], 2, xb, ny, nz) for l in range(1, LEVELS)]
-    scratch += [vm(2, xr[l], ny, nz) for l in range(1, LEVELS)]
-    scratch += [vm(2, xr[l], ny, nz) for l in range(1, LEVELS - 1)]
-    scratch += [dma((3 + 2 * C + 1,)), dma((2 * C,)), dma((6,)), dma((6,)), dma((2, 6 * C)), dma((2, 6 * C)),
+    scratch += [vm(times[l], 2, xr[l], ny, nz) for l in range(2, LEVELS)]
+    scratch += [vm(times[l], 2, xb, ny, nz) for l in range(2, LEVELS)]
+    scratch += [vm(2, xr[l], ny, nz) for l in range(2, LEVELS)]
+    scratch += [vm(2, xr[l], ny, nz) for l in range(2, LEVELS - 1)]
+    scratch += [dma((3 + 2 * C + 1,)), dma((2 * C,)), dma((6,)), dma((6,)), dma((2, NP * C)), dma((2, NP * C)),
                 dma((2 * C + 1,)), dma((2 * C + 1,)), dma((group,)), dma((group,)), dma((2, group)), dma((2, group)),
-                dma((2, n_x)), dma((2, n_x)), dma((1,)), dma((1,)), dma((n_t,)), dma((n_t,)), dma((2 * C,)), dma((2 * C,))]
+                dma((2, n_x)), dma((2, n_x)), dma((2, group)), dma((2, group)), dma((n_t,)), dma((n_t,)),
+                dma((2 * C,)), dma((2 * C,)), dma((group,)), dma((group,)), dma((2, group)), dma((2, group))]
     shape = jax.ShapeDtypeStruct((nt, nx, ny, nz), F32)
     anyspec = pl.BlockSpec(memory_space=pl.ANY)
     return pl.pallas_call(

time: 156 us -> 146 us (0.936); the launches traced: 153 us -> 146 us
  Pallas kernels: 149 us -> 142 us
    pallas_call x1, Pallas kernels: 149 us -> 142 us  [body(): return make(mesh, *source.shape)(source, initial_guess, diffusivity)]
where the time goes in v2:
time: 146 us
  Pallas kernels  142 us (97%)
  local copies, waits for them, and re-layouts  3.32 us (2%)
    pallas_call x1, Pallas kernels, body(): return make(mesh, *source.shape)(source, initial_guess, diffusivity)  142 us
    unnamed x4, local copies, waits for them, and re-layouts  3.32 us

profile of v2, /device:TPU:25, one launch (start us, length us, event | category | flops | bytes accessed | tf_op | source)
XLA Modules:
  0.0 146.0 jit_solution(9805633632320215542)
XLA Ops:
  0.6 142.0 %shard_map.50 = (f32[2,32,32,128]{3,2,1,0:T(8,128)}, f32[2,32,32,128]{3,2,1,0:T(8,128)}) custom-call(f32[2,32,32,128]{3,2,1,0:T(8,128)} %src.1, f32[2,32,32,128]{3,2,1,0:T(8,128)} %guess.1, f32[32,32,128]{2,1,0:T(8,128)} %dif_hbm.1), custom_call_target="tpu_custom_call" | custom-call | tf_op jit(solution)/shard_map/pallas_call | solution.py:784
  142.7 0.0 copy-start
  142.7 2.4 %copy.7 = f32[2,32,32,128]{3,2,1,0:T(8,128)} copy(f32[2,32,32,128]{3,2,1,0:T(8,128)} %get-tuple-element.4) | data formatting | bytes 2097152
  145.0 0.0 copy-done
  145.1 1.0 copy.8
Async XLA Ops:
  142.7 2.4 %copy-start = (f32[2,32,32,128]{3,2,1,0:T(8,128)S(1)}, f32[2,32,32,128]{3,2,1,0:T(8,128)}, u32[]{:S(2)}) copy-start(f32[2,32,32,128]{3,2,1,0:T(8,128)} %get-tuple-element.5) | copy-start | bytes 3145732

commit v3 on v2

--- a/solution.py
+++ b/solution.py
@@ -17,6 +17,7 @@
 D0 = 8
 D1 = 16
 NP = 10
+OWN_ONLY = (4, 9)
 
 
 def make(mesh, nt, nx, ny, nz):
@@ -28,7 +29,7 @@
     xp = nx + 2 * PX
     rb = LANES // ny
     q = nx // 8
-    cuts = {"down": [0, 2 * q, 4 * q, 6 * q, nx], "up": [0, 2 * q, 4 * q, 6 * q, nx]}
+    cuts = {"down": [0, 2 * q, 4 * q, 6 * q, nx], "up": [0, 2 * q, 5 * q, 7 * q, nx]}
     C = len(cuts["down"]) - 1
     nblk = nx // rb
     times = [0] + [group // 2**l for l in range(LEVELS - 1)]
@@ -378,8 +379,9 @@
                 PSs[n, block0(j) + b, pl.ds(D0, D0)] = hi8
             own, halo = d_copies(n, v, t, j, off)
             start(I < ntm - 1, own)
-            each(m // rb, fn, 3)
-            start(I < ntm - 1, halo)
+            if n not in OWN_ONLY:
+                each(m // rb, fn, 3)
+                start(I < ntm - 1, halo)
 
         def d_recv(n, v, t, j, off):
             lo, m = span(j, off)
@@ -388,6 +390,8 @@
             @pl.when(I > 0)
             def _():
                 own.wait_recv()
+                if n in OWN_ONLY:
+                    return
                 halo.wait_recv()
 
                 def fn(b):
@@ -690,16 +694,16 @@
                 near.start()
             outs.append((far, near))
 
-        def emit_sol(j):
+        def emit_sol(j, t):
             lo, hi = inside(j, 4)
-            emit(VB.at[:, 0, pl.ds(PX + lo, hi - lo), center], sol.at[:, pl.ds(lo, hi - lo)], j)
+            emit(VB.at[t, 0, pl.ds(PX + lo, hi - lo), center], sol.at[t, pl.ds(lo, hi - lo)], t * C + j)
 
         def put_r(x, rs):
             for t in range(nt):
                 rout[t, x] = rs[t][0]
 
         def emit_res(j, lo, hi):
-            emit(rout.at[:, pl.ds(lo, hi - lo)], res.at[:, pl.ds(lo, hi - lo)], C + j)
+            emit(rout.at[:, pl.ds(lo, hi - lo)], res.at[:, pl.ds(lo, hi - lo)], nt * C + j)
 
         for j in range(C + 4):
             if 0 <= j - 4 < C:
@@ -714,10 +718,11 @@
                 relax(fine, VC, VA, 0, PV[7], *span(k, 3))
                 for t in before:
                     relax(fine, VA, VB, t, None, *span(k, 4))
+                    emit_sol(k, t)
                 d_send(9, VB, last, k, 4)
                 d_recv(8, VA, last, k, 3)
                 relax(fine, VA, VB, 0, PV[8], *span(k, 4))
-                emit_sol(k)
+                emit_sol(k, 0)
             if 0 <= j - 2 < C:
                 k = j - 2
                 d_recv(6, WA, 0, k, 1)
@@ -763,10 +768,10 @@
     scratch += [vm(times[l], 2, xb, ny, nz) for l in range(2, LEVELS)]
     scratch += [vm(2, xr[l], ny, nz) for l in range(2, LEVELS)]
     scratch += [vm(2, xr[l], ny, nz) for l in range(2, LEVELS - 1)]
-    scratch += [dma((3 + 2 * C + 1,)), dma((2 * C,)), dma((6,)), dma((6,)), dma((2, NP * C)), dma((2, NP * C)),
+    scratch += [dma((3 + 2 * C + 1,)), dma(((nt + 1) * C,)), dma((6,)), dma((6,)), dma((2, NP * C)), dma((2, NP * C)),
                 dma((2 * C + 1,)), dma((2 * C + 1,)), dma((group,)), dma((group,)), dma((2, group)), dma((2, group)),
                 dma((2, n_x)), dma((2, n_x)), dma((2, group)), dma((2, group)), dma((n_t,)), dma((n_t,)),
-                dma((2 * C,)), dma((2 * C,)), dma((group,)), dma((group,)), dma((2, group)), dma((2, group))]
+                dma(((nt + 1) * C,)), dma(((nt + 1) * C,)), dma((group,)), dma((group,)), dma((2, group)), dma((2, group))]
     shape = jax.ShapeDtypeStruct((nt, nx, ny, nz), F32)
     anyspec = pl.BlockSpec(memory_space=pl.ANY)
     return pl.pallas_call(

time: 146 us -> 144 us (0.986)
  Pallas kernels: 142 us -> 140 us
    pallas_call x1, Pallas kernels: 142 us -> 140 us  [body(): return make(mesh, *source.shape)(source, initial_guess, diffusivity)]
where the time goes in v3:
time: 144 us
  Pallas kernels  140 us (97%)
  local copies, waits for them, and re-layouts  3.32 us (2%)
    pallas_call x1, Pallas kernels, body(): return make(mesh, *source.shape)(source, initial_guess, diffusivity)  140 us
    unnamed x4, local copies, waits for them, and re-layouts  3.32 us

profile of v3, /device:TPU:25, one launch (start us, length us, event | category | flops | bytes accessed | tf_op | source)
XLA Modules:
  0.0 143.9 jit_solution(16399571605562172399)
XLA Ops:
  0.6 140.0 %shard_map.50 = (f32[2,32,32,128]{3,2,1,0:T(8,128)}, f32[2,32,32,128]{3,2,1,0:T(8,128)}) custom-call(f32[2,32,32,128]{3,2,1,0:T(8,128)} %src.1, f32[2,32,32,128]{3,2,1,0:T(8,128)} %guess.1, f32[32,32,128]{2,1,0:T(8,128)} %dif_hbm.1), custom_call_target="tpu_custom_call" | custom-call | tf_op jit(solution)/shard_map/pallas_call | solution.py:789
  140.6 0.0 copy-start
  140.6 2.4 %copy.7 = f32[2,32,32,128]{3,2,1,0:T(8,128)} copy(f32[2,32,32,128]{3,2,1,0:T(8,128)} %get-tuple-element.4) | data formatting | bytes 2097152
  143.0 0.0 copy-done
  143.0 1.0 copy.8
Async XLA Ops:
  140.6 2.4 %copy-start = (f32[2,32,32,128]{3,2,1,0:T(8,128)S(1)}, f32[2,32,32,128]{3,2,1,0:T(8,128)}, u32[]{:S(2)}) copy-start(f32[2,32,32,128]{3,2,1,0:T(8,128)} %get-tuple-element.5) | copy-start | bytes 3145732
